TPU v7x, 32 devices: a whole 2x2x4 slice. The times are simulated.
32 devices in a mesh: face: 2 (over y), fy: 4 (over x, core), fx: 4 (over z).
Axes of the slice: x: 2, y: 2, z: 4, core: 2. Of those that a mesh axis runs over, the one named last changes fastest.
Arguments:
- state: float32 [6, 32, 32, 192], P('face', 'fy', 'fx'), may hold values from -6 to 6
- jacobian: float32 [6, 32, 32], P('face', 'fy', 'fx'), may hold values from 0.5 to 2
- metric_diag: float32 [2, 6, 32, 32], P(None, 'face', 'fy', 'fx'), may hold values from 0.6 to 1.4
- metric_cross: float32 [6, 32, 32], P('face', 'fy', 'fx'), may hold values from -0.3 to 0.3
- coriolis: float32 [6, 32, 32], P('face', 'fy', 'fx'), may hold values from -2 to 2
- nbr_face: int32 [6, 4], replicated, may hold values from 0 to 5, as said below
- nbr_edge: int32 [6, 4], replicated, may hold values from 0 to 3, as said below
Outputs:
- updated: float32 [6, 32, 32, 192], P('face', 'fy', 'fx')
Inputs may be any that keep to these rules, and one draw needn't show every extreme that they name: Edge e of a face is 0 south (row 0), 1 east (last column), 2 north (last row), 3 west (column 0). Edge e of face f is glued to edge nbr_edge[f, e] of face nbr_face[f, e], and that edge back to it; the 6 faces are glued as the surface of a cube, three faces at each corner, the two glued edges running in opposite senses when both are read counterclockwise. `nbr_edge`: see nbr_face.
All inputs are finite; a program needn't handle non-finite values.
Results may differ from a plain program's by a relative error of at most 0.0001.
Values sent between devices are 32-bit elements; how exact they have to be, the bound alone decides.
A program may use at most 64 MiB of HBM per device.

v0:
```python
import jax
import jax.numpy as jnp
import numpy as np
from jax import lax
from jax.sharding import PartitionSpec as P

time_step = 0.05
hyper_coeff = 0.0005


def padded(cells, sides, width):
    for axis, dim in sides:
        count = lax.axis_size(axis)
        ends = count - 1
        head = lax.slice_in_dim(cells, 0, width, axis=dim)
        tail = lax.slice_in_dim(cells, cells.shape[dim] - width, cells.shape[dim], axis=dim)
        cells = jnp.concatenate(
            [
                lax.ppermute(tail, axis, [(i, (i + 1) % count) for i in range(ends)]),
                cells,
                lax.ppermute(head, axis, [((i + 1) % count, i) for i in range(ends)]),
            ],
            axis=dim,
        )
    return cells


def deriv_table():
    gll_nodes = np.array([-1.0, -1.0 / np.sqrt(5.0), 1.0 / np.sqrt(5.0), 1.0])
    bary_weights = np.ones(4)
    for j in range(4):
        for m in range(4):
            if m != j:
                bary_weights[j] = bary_weights[j] / (gll_nodes[j] - gll_nodes[m])
    matrix = np.zeros((4, 4))
    for i in range(4):
        for j in range(4):
            if i != j:
                matrix[i, j] = bary_weights[j] / bary_weights[i] / (gll_nodes[i] - gll_nodes[j])
        matrix[i, i] = -np.sum(matrix[i])
    return matrix


def along_x(values):
    face_count, row_count, col_count, chan_count = values.shape
    blocks = values.reshape(face_count, row_count, col_count // 4, 4, chan_count)
    result = jnp.einsum(
        "jk,abekc->abejc",
        jnp.asarray(deriv_table(), jnp.float32),
        blocks,
        precision=lax.Precision.HIGHEST,
    )
    return result.reshape(values.shape)


def along_y(values):
    face_count, row_count, col_count, chan_count = values.shape
    blocks = values.reshape(face_count, row_count // 4, 4, col_count, chan_count)
    result = jnp.einsum(
        "ik,aekxc->aeixc",
        jnp.asarray(deriv_table(), jnp.float32),
        blocks,
        precision=lax.Precision.HIGHEST,
    )
    return result.reshape(values.shape)


def mass_of(jacobian):
    weights = jnp.asarray([1.0 / 6.0, 5.0 / 6.0, 5.0 / 6.0, 1.0 / 6.0], jnp.float32)
    row_weight = jnp.tile(weights, jacobian.shape[1] // 4)
    col_weight = jnp.tile(weights, jacobian.shape[2] // 4)
    return jacobian * row_weight[None, :, None] * col_weight[None, None, :]


def tendency(state, geometry, planet):
    volume, metric_xx, metric_yy, metric_xy = geometry
    levels = state.shape[-1] // 3
    wind_u = state[..., :levels]
    wind_v = state[..., levels : 2 * levels]
    temper = state[..., 2 * levels :]
    contra_u = metric_xx * wind_u + metric_xy * wind_v
    contra_v = metric_xy * wind_u + metric_yy * wind_v
    energy = 0.5 * (wind_u * contra_u + wind_v * contra_v) + temper
    xderivs = along_x(jnp.concatenate([wind_v, temper, energy], -1))
    yderivs = along_y(jnp.concatenate([wind_u, temper, energy], -1))
    absolute = (xderivs[..., :levels] - yderivs[..., :levels]) / volume + planet
    tend_u = absolute * volume * contra_v - xderivs[..., 2 * levels :]
    tend_v = -absolute * volume * contra_u - yderivs[..., 2 * levels :]
    tend_t = -(
        contra_u * xderivs[..., levels : 2 * levels] + contra_v * yderivs[..., levels : 2 * levels]
    )
    return state + time_step * jnp.concatenate([tend_u, tend_v, tend_t], -1)


def laplace(values, geometry):
    volume, metric_xx, metric_yy, metric_xy = geometry
    grad_x = along_x(values)
    grad_y = along_y(values)
    flux_x = volume * (metric_xx * grad_x + metric_xy * grad_y)
    flux_y = volume * (metric_xy * grad_x + metric_yy * grad_y)
    return (along_x(flux_x) + along_y(flux_y)) / volume


def combine(values, axis):
    length = values.shape[axis] - 2
    positions = jnp.arange(length)
    leading = (positions % 4 == 0).astype(jnp.float32)
    trailing = (positions % 4 == 3).astype(jnp.float32)
    broad_shape = [1, 1, 1, 1]
    broad_shape[axis] = length
    leading = leading.reshape(broad_shape)
    trailing = trailing.reshape(broad_shape)
    middle = lax.slice_in_dim(values, 1, length + 1, axis=axis)
    previous = lax.slice_in_dim(values, 0, length, axis=axis)
    following = lax.slice_in_dim(values, 2, length + 2, axis=axis)
    return middle + leading * previous + trailing * following


def rotate(segment, quarter, levels):
    cosine = ((quarter == 0).astype(jnp.float32) - (quarter == 2).astype(jnp.float32))[..., None]
    sine_part = ((quarter == 1).astype(jnp.float32) - (quarter == 3).astype(jnp.float32))[..., None]
    wind_u = segment[..., :levels]
    wind_v = segment[..., levels : 2 * levels]
    return jnp.concatenate(
        [
            cosine * wind_u - sine_part * wind_v,
            sine_part * wind_u + cosine * wind_v,
            segment[..., 2 * levels :],
        ],
        -1,
    )


def in_face(values):
    across = combine(padded(values, (("fx", 2),), 1), 2)
    return combine(padded(across, (("fy", 1),), 1), 1)


def place_pieces(
    got_flat,
    got_tall,
    vector,
    nbr_edge,
    flat_edge,
    tall_edge,
    on_south,
    on_west,
    flat_start,
    tall_start,
    face_local,
    side_nodes,
    chan_count,
    levels,
):
    edge_ids = jnp.arange(4, dtype=jnp.int32)
    flat_target = nbr_edge[:, flat_edge]
    tall_target = nbr_edge[:, tall_edge]
    if vector:
        got_flat = rotate(got_flat, ((flat_target - flat_edge + 2) % 4)[None, :, None], levels)
        got_tall = rotate(got_tall, ((tall_target - tall_edge + 2) % 4)[None, :, None], levels)
    got_flat = jnp.where(on_south, got_flat[:, :, ::-1], got_flat)
    got_tall = jnp.where(on_west, got_tall, got_tall[:, :, ::-1])
    flat_pick = (flat_target[:, None] == edge_ids[None, :]).astype(jnp.float32)
    tall_pick = (tall_target[:, None] == edge_ids[None, :]).astype(jnp.float32)
    flat_rims = jnp.einsum("se,gsjc->gejc", flat_pick, got_flat, precision=lax.Precision.HIGHEST)
    tall_rims = jnp.einsum("se,gsjc->gejc", tall_pick, got_tall, precision=lax.Precision.HIGHEST)
    empty_rims = jnp.zeros((face_local, 4, side_nodes, chan_count), jnp.float32)
    rim_strips = lax.dynamic_update_slice(empty_rims, flat_rims, (0, 0, flat_start, 0))
    return rim_strips + lax.dynamic_update_slice(empty_rims, tall_rims, (0, 0, tall_start, 0))


def outgoing(
    summed, nbr_face, face_ids, flat_edge, tall_edge, on_south, on_west, flat_live, tall_live
):
    row_count = summed.shape[1]
    col_count = summed.shape[2]
    all_faces = jnp.arange(nbr_face.shape[0], dtype=jnp.int32)
    flat_piece = jnp.where(on_south, summed[:, 0], summed[:, row_count - 1])
    tall_piece = jnp.where(on_west, summed[:, :, 0], summed[:, :, col_count - 1])
    flat_dest = nbr_face[face_ids, flat_edge]
    tall_dest = nbr_face[face_ids, tall_edge]
    flat_send = ((all_faces[:, None] == flat_dest[None, :]) & flat_live).astype(jnp.float32)
    tall_send = ((all_faces[:, None] == tall_dest[None, :]) & tall_live).astype(jnp.float32)
    return (
        flat_send[:, :, None, None] * flat_piece[None],
        tall_send[:, :, None, None] * tall_piece[None],
    )


def assemble(values, vector, nbr_face, nbr_edge):
    summed = in_face(values)
    face_local, row_count, col_count, chan_count = summed.shape
    levels = chan_count // 3
    row_index = lax.axis_index("fy")
    col_index = lax.axis_index("fx")
    side_nodes = row_count * lax.axis_size("fy")
    face_ids = lax.axis_index("face") * face_local + jnp.arange(face_local, dtype=jnp.int32)
    on_south = row_index == 0
    on_north = row_index == lax.axis_size("fy") - 1
    on_west = col_index == 0
    on_east = col_index == lax.axis_size("fx") - 1
    flat_live = on_south | on_north
    tall_live = on_west | on_east
    flat_edge = jnp.where(on_south, 0, 2).astype(jnp.int32)
    tall_edge = jnp.where(on_west, 3, 1).astype(jnp.int32)
    flat_start = jnp.where(
        on_south, side_nodes - (col_index + 1) * col_count, col_index * col_count
    )
    tall_start = jnp.where(on_west, row_index * row_count, side_nodes - (row_index + 1) * row_count)
    send_flat, send_tall = outgoing(
        summed, nbr_face, face_ids, flat_edge, tall_edge, on_south, on_west, flat_live, tall_live
    )
    got_flat, got_tall = (
        lax.all_to_all(send_flat, "face", split_axis=0, concat_axis=1, tiled=True),
        lax.all_to_all(send_tall, "face", split_axis=0, concat_axis=1, tiled=True),
    )
    rim_strips = place_pieces(
        got_flat,
        got_tall,
        vector,
        nbr_edge,
        flat_edge,
        tall_edge,
        on_south,
        on_west,
        flat_start,
        tall_start,
        face_local,
        side_nodes,
        chan_count,
        levels,
    )
    flat_lines = jnp.stack([rim_strips[:, 0], rim_strips[:, 2, ::-1]], axis=1)
    flat_lines = flat_lines.reshape(face_local, 2, lax.axis_size("fx"), col_count, chan_count)
    tall_lines = jnp.stack([rim_strips[:, 1], rim_strips[:, 3, ::-1]], axis=1)
    tall_lines = tall_lines.reshape(face_local, 2, lax.axis_size("fy"), row_count, chan_count)
    flat_whole = lax.psum(flat_lines, "fy")
    tall_whole = lax.psum(tall_lines, "fx")
    flat_block = lax.psum_scatter(flat_whole, "fx", scatter_dimension=2, tiled=True)
    tall_block = lax.psum_scatter(tall_whole, "fy", scatter_dimension=2, tiled=True)
    flat_add = jnp.where(on_south, flat_block[:, 0, 0], flat_block[:, 1, 0])
    tall_add = jnp.where(on_west, tall_block[:, 1, 0], tall_block[:, 0, 0])
    result = summed.at[:, 0].add(jnp.where(on_south, flat_add, 0.0))
    result = result.at[:, row_count - 1].add(jnp.where(on_north, flat_add, 0.0))
    result = result.at[:, :, 0].add(jnp.where(on_west, tall_add, 0.0))
    result = result.at[:, :, col_count - 1].add(jnp.where(on_east, tall_add, 0.0))
    return result


def per_device(state, jacobian, metric_diag, metric_cross, coriolis, nbr_face, nbr_edge):
    node_mass = mass_of(jacobian)[..., None]
    total_mass = assemble(node_mass, False, nbr_face, nbr_edge)
    geometry = (
        jacobian[..., None],
        metric_diag[0][..., None],
        metric_diag[1][..., None],
        metric_cross[..., None],
    )
    raw = tendency(state, geometry, coriolis[..., None])
    sectioned = assemble(node_mass * raw, True, nbr_face, nbr_edge) / total_mass
    first_lap = (
        assemble(node_mass * laplace(sectioned, geometry), True, nbr_face, nbr_edge) / total_mass
    )
    second_lap = (
        assemble(node_mass * laplace(first_lap, geometry), True, nbr_face, nbr_edge) / total_mass
    )
    return sectioned - hyper_coeff * second_lap


def solution(mesh):
    return jax.shard_map(
        per_device,
        mesh=mesh,
        in_specs=(
            P("face", "fy", "fx", None),
            P("face", "fy", "fx"),
            P(None, "face", "fy", "fx"),
            P("face", "fy", "fx"),
            P("face", "fy", "fx"),
            P(),
            P(),
        ),
        out_specs=P("face", "fy", "fx", None),
        check_vma=False,
    )
```

profile of v0, /device:TPU:0, one launch (start us, length us, event | category | flops | bytes accessed | tf_op | source)
XLA Modules:
  0.0 370.9 jit_solution(3466996314126042414)
XLA Ops:
  7.4 0.8 fusion.161
  8.1 1.0 slice.770
  13.0 1.3 collective-permute-start.1
  14.4 5.6 %collective-permute-start = (f32[3,8,1,192]{3,2,0,1:T(1,128)S(1)}, f32[3,8,1,192]{3,2,0,1:T(1,128)S(1)}, u32[]{:S(2)}, u32[]{:S(2)}) collective-permute-start(f32[3,8,1,192]{3,2,0,1:T(1,128)S(1)} %slice.902), channel_id=1, source_target_pairs={{0,1},{1,2},{2,3},{4,5},{5,6},{6,7},{8,9},{9,10},{10,11},{12,13},{... | collective-permute-start | bytes 55304 | tf_op jit(solution)/shard_map/ppermute | solution.py:19
  20.1 1.3 collective-permute-start.5
  21.4 4.5 %collective-permute-start.4 = (f32[3,8,1,1]{2,1,0,3:T(8,128)S(1)}, f32[3,8,1,1]{2,1,0,3:T(8,128)S(1)}, u32[]{:S(2)}, u32[]{:S(2)}) collective-permute-start(f32[3,8,1,1]{2,1,0,3:T(8,128)S(1)} %get-tuple-element.262), channel_id=1, source_target_pairs={{0,1},{1,2},{2,3},{4,5},{5,6},{6,7},{8,9},{9,10},{10,11},{12,13},{... | collective-permute-start | bytes 296 | tf_op jit(solution)/shard_map/ppermute | solution.py:19
  31.1 1.3 collective-permute-start.7
  32.4 3.0 collective-permute-start.6
  35.5 0.8 collective-permute-done.6
  37.2 3.2 all-to-all-start.2
  41.1 3.1 all-to-all-done.2
  44.3 3.2 all-to-all-start.3
  47.6 3.7 all-to-all-done.3
  52.8 1.3 collective-permute-start.3
  54.1 3.0 collective-permute-start.2
  57.2 13.3 %all-reduce.4 = f32[3,2,4,8,1]{3,1,4,0,2:T(2,128)S(1)} all-reduce(f32[3,2,4,8,1]{3,1,4,0,2:T(2,128)S(1)} %copy.284), channel_id=5, replica_groups=mesh['face'=2,'fy'=4,'fx'=4] {'fy'}, use_global_device_ids=true, to_apply=%region_7.8.clone | all-reduce | flops 192 | bytes 1536
  70.7 0.7 broadcast_multiply_fusion.5
  71.4 3.4 all-to-all-start
  74.9 0.8 broadcast_multiply_fusion.4
  75.7 3.7 %all-to-all-done = f32[6,3,8,192]{3,2,1,0:T(8,128)S(1)} async-done(((f32[6,3,8,192]{3,2,1,0:T(8,128)}), f32[6,3,8,192]{3,2,1,0:T(8,128)S(1)}, u32[]{:S(2)}, u32[]{:S(2)}) %all-to-all-start) | async-done | bytes 110624 | tf_op jit(solution)/shard_map/all_to_all | solution.py:214
  79.4 3.4 all-to-all-start.1
  83.3 4.1 %all-to-all-done.1 = f32[6,3,8,192]{3,2,1,0:T(8,128)S(1)} async-done(((f32[6,3,8,192]{3,2,1,0:T(8,128)}), f32[6,3,8,192]{3,2,1,0:T(8,128)S(1)}, u32[]{:S(2)}, u32[]{:S(2)}) %all-to-all-start.1) | async-done | bytes 110624 | tf_op jit(solution)/shard_map/all_to_all | solution.py:215
  88.9 0.7 copy.270
  91.5 33.0 %all-reduce.13.cloned.1.call-done = f32[3,2,4,8,192]{4,3,0,2,1:T(8,128)} async-done(((f32[3,2,4,8,192]{4,3,0,2,1:T(8,128)}), f32[3,2,4,8,192]{4,3,0,2,1:T(8,128)}) %all-reduce.13.cloned.1.call-update) | async-done | bytes 147472
  124.5 1.4 constant_dynamic-slice_fusion.6
  125.9 0.8 copy.277
  126.8 18.5 %all-reduce.7 = (f32[3,2,1,8,192]{4,1,3,2,0:T(2,128)S(1)}, f32[3,2,4,8,1]{3,1,4,0,2:T(2,128)S(1)}, f32[3,2,1,8,1]{3,1,4,0,2:T(2,128)S(1)}) all-reduce(f32[3,2,1,8,192]{4,1,3,2,0:T(2,128)S(1)} %copy.277, f32[3,2,4,8,1]{3,1,4,0,2:T(2,128)S(1)} %copy.281, ...), channel_id=1, replica_groups=mesh['face'=2,'fy'=4,'fx'=4] {'fx'}, use_global_device_ids=true, to_apply=%region_2.3 | all-reduce | flops 9456 | bytes 75648 | tf_op jit(solution)/shard_map/psum | solution.py:238
  145.9 10.7 %all-reduce.8 = (f32[3,2,1,8,192]{4,3,0,2,1:T(8,128)S(1)}, f32[3,2,1,8,1]{3,1,4,0,2:T(2,128)S(1)}) all-reduce(f32[3,2,1,8,192]{4,3,0,2,1:T(8,128)S(1)} %constant_dynamic-slice_fusion.6, f32[3,2,1,8,1]{3,1,4,0,2:T(2,128)S(1)} %constant_dynamic-slice_fusion.5), channel_id=1, replica_groups=mesh['face'=2,'fy'=4,'fx'=4] {'fy'}, use_global_device_ids=true, to_apply=%region_0.1 | all-reduce | flops 9264 | bytes 74112 | tf_op jit(solution)/shard_map/psum | solution.py:237
  160.6 1.3 collective-permute-start.9
  161.9 4.5 %collective-permute-start.8 = (f32[3,8,1,192]{3,2,0,1:T(1,128)S(1)}, f32[3,8,1,192]{3,2,0,1:T(1,128)S(1)}, u32[]{:S(2)}, u32[]{:S(2)}) collective-permute-start(f32[3,8,1,192]{3,2,0,1:T(1,128)S(1)} %get-tuple-element.230), channel_id=1, source_target_pairs={{0,1},{1,2},{2,3},{4,5},{5,6},{6,7},{8,9},{9,10},{10,11},{12,13},{... | collective-permute-start | bytes 55304 | tf_op jit(solution)/shard_map/ppermute | solution.py:19
  166.4 1.5 collective-permute-done.8
  168.0 1.3 collective-permute-start.11
  169.3 3.2 collective-permute-start.10
  173.4 0.7 broadcast_multiply_fusion.3
  174.1 3.4 all-to-all-start.4
  177.6 0.8 broadcast_multiply_fusion.2
  178.3 4.0 %all-to-all-done.4 = f32[6,3,8,192]{3,2,1,0:T(8,128)S(1)} async-done(((f32[6,3,8,192]{3,2,1,0:T(8,128)}), f32[6,3,8,192]{3,2,1,0:T(8,128)S(1)}, u32[]{:S(2)}, u32[]{:S(2)}) %all-to-all-start.4) | async-done | bytes 110624 | tf_op jit(solution)/shard_map/all_to_all | solution.py:214
  182.3 3.4 all-to-all-start.5
  186.2 4.3 %all-to-all-done.5 = f32[6,3,8,192]{3,2,1,0:T(8,128)S(1)} async-done(((f32[6,3,8,192]{3,2,1,0:T(8,128)}), f32[6,3,8,192]{3,2,1,0:T(8,128)S(1)}, u32[]{:S(2)}, u32[]{:S(2)}) %all-to-all-start.5) | async-done | bytes 110624 | tf_op jit(solution)/shard_map/all_to_all | solution.py:215
  192.1 0.7 copy.308
  193.8 35.0 %all-reduce.15.cloned.1.call-done = f32[3,2,4,8,192]{4,3,0,2,1:T(8,128)} async-done(((f32[3,2,4,8,192]{4,3,0,2,1:T(8,128)}), f32[3,2,4,8,192]{4,3,0,2,1:T(8,128)}) %all-reduce.15.cloned.1.call-update) | async-done | bytes 147472
  228.8 1.4 constant_dynamic-slice_fusion.3
  230.3 10.5 %psum.68 = f32[3,2,1,8,192]{4,3,0,2,1:T(8,128)S(1)} all-reduce(f32[3,2,1,8,192]{4,3,0,2,1:T(8,128)S(1)} %constant_dynamic-slice_fusion.3), channel_id=1, replica_groups=mesh['face'=2,'fy'=4,'fx'=4] {'fy'}, use_global_device_ids=true, to_apply=%region_8.9 | all-reduce | flops 9216 | bytes 73728 | tf_op jit(solution)/shard_map/psum | solution.py:237
  240.9 0.8 copy.314
  241.7 18.2 %psum.69 = f32[3,2,1,8,192]{4,1,3,2,0:T(2,128)S(1)} all-reduce(f32[3,2,1,8,192]{4,1,3,2,0:T(2,128)S(1)} %copy.314), channel_id=1, replica_groups=mesh['face'=2,'fy'=4,'fx'=4] {'fx'}, use_global_device_ids=true, to_apply=%region_10.11 | all-reduce | flops 9216 | bytes 73728 | tf_op jit(solution)/shard_map/psum | solution.py:238
  263.2 1.3 collective-permute-start.13
  264.5 4.5 %collective-permute-start.12 = (f32[3,8,1,192]{3,2,0,1:T(1,128)S(1)}, f32[3,8,1,192]{3,2,0,1:T(1,128)S(1)}, u32[]{:S(2)}, u32[]{:S(2)}) collective-permute-start(f32[3,8,1,192]{3,2,0,1:T(1,128)S(1)} %get-tuple-element.226), channel_id=1, source_target_pairs={{0,1},{1,2},{2,3},{4,5},{5,6},{6,7},{8,9},{9,10},{10,11},{12,13},{... | collective-permute-start | bytes 55304 | tf_op jit(solution)/shard_map/ppermute | solution.py:19
  269.0 1.5 collective-permute-done.12
  270.6 1.3 collective-permute-start.15
  271.9 3.0 collective-permute-start.14
  275.0 0.8 collective-permute-done.14
  276.0 0.7 broadcast_multiply_fusion.1
  276.7 3.4 all-to-all-start.6
  280.2 0.8 broadcast_multiply_fusion
  280.9 4.0 %all-to-all-done.6 = f32[6,3,8,192]{3,2,1,0:T(8,128)S(1)} async-done(((f32[6,3,8,192]{3,2,1,0:T(8,128)}), f32[6,3,8,192]{3,2,1,0:T(8,128)S(1)}, u32[]{:S(2)}, u32[]{:S(2)}) %all-to-all-start.6) | async-done | bytes 110624 | tf_op jit(solution)/shard_map/all_to_all | solution.py:214
  284.9 3.4 all-to-all-start.7
  288.9 4.2 %all-to-all-done.7 = f32[6,3,8,192]{3,2,1,0:T(8,128)S(1)} async-done(((f32[6,3,8,192]{3,2,1,0:T(8,128)}), f32[6,3,8,192]{3,2,1,0:T(8,128)S(1)}, u32[]{:S(2)}, u32[]{:S(2)}) %all-to-all-start.7) | async-done | bytes 110624 | tf_op jit(solution)/shard_map/all_to_all | solution.py:215
  294.7 0.7 copy.326
  296.4 34.9 %all-reduce.17.cloned.1.call-done = f32[3,2,4,8,192]{4,3,0,2,1:T(8,128)} async-done(((f32[3,2,4,8,192]{4,3,0,2,1:T(8,128)}), f32[3,2,4,8,192]{4,3,0,2,1:T(8,128)}) %all-reduce.17.cloned.1.call-update) | async-done | bytes 147472
  331.3 1.4 constant_dynamic-slice_fusion.2
  332.8 10.5 %psum.70 = f32[3,2,1,8,192]{4,3,0,2,1:T(8,128)S(1)} all-reduce(f32[3,2,1,8,192]{4,3,0,2,1:T(8,128)S(1)} %constant_dynamic-slice_fusion.2), channel_id=1, replica_groups=mesh['face'=2,'fy'=4,'fx'=4] {'fy'}, use_global_device_ids=true, to_apply=%region_12.13 | all-reduce | flops 9216 | bytes 73728 | tf_op jit(solution)/shard_map/psum | solution.py:237
  343.4 0.8 copy.330
  344.2 18.2 %psum.71 = f32[3,2,1,8,192]{4,1,3,2,0:T(2,128)S(1)} all-reduce(f32[3,2,1,8,192]{4,1,3,2,0:T(2,128)S(1)} %copy.330), channel_id=1, replica_groups=mesh['face'=2,'fy'=4,'fx'=4] {'fx'}, use_global_device_ids=true, to_apply=%region_14.15 | all-reduce | flops 9216 | bytes 73728 | tf_op jit(solution)/shard_map/psum | solution.py:238
  362.8 0.8 multiply_subtract_fusion
  (252 shorter events, 31.3 us)
Async XLA Ops:
  7.4 19.6 %copy-start = (s32[6,4]{0,1:T(4,128)S(1)}, s32[6,4]{0,1:T(4,128)}, u32[]{:S(2)}) copy-start(s32[6,4]{0,1:T(4,128)} %param.55) | copy-start | bytes 292
  7.4 1.8 copy-start.1
  8.1 1.0 copy-start.3
  9.5 0.7 copy-start.4
  11.2 0.7 copy-start.9
  11.2 0.7 copy-start.2
  12.0 0.7 copy-start.5
  13.0 39.6 %collective-permute-start.1 = (f32[3,8,1,192]{3,2,1,0:T(1,128)S(1)}, f32[3,8,1,192]{3,2,1,0:T(1,128)S(1)}, u32[]{:S(2)}, u32[]{:S(2)}) collective-permute-start(f32[3,8,1,192]{3,2,1,0:T(1,128)S(1)} %slice.903), channel_id=1, source_target_pairs={{1,0},{2,1},{3,2},{5,4},{6,5},{7,6},{9,8},{10,9},{11,10},{13,12},{... | collective-permute-start | bytes 55304 | tf_op jit(solution)/shard_map/ppermute | solution.py:21
  14.4 38.2 %collective-permute-start = (f32[3,8,1,192]{3,2,0,1:T(1,128)S(1)}, f32[3,8,1,192]{3,2,0,1:T(1,128)S(1)}, u32[]{:S(2)}, u32[]{:S(2)}) collective-permute-start(f32[3,8,1,192]{3,2,0,1:T(1,128)S(1)} %slice.902), channel_id=1, source_target_pairs={{0,1},{1,2},{2,3},{4,5},{5,6},{6,7},{8,9},{9,10},{10,11},{12,13},{... | collective-permute-start | bytes 55304 | tf_op jit(solution)/shard_map/ppermute | solution.py:19
  20.1 10.9 %collective-permute-start.5 = (f32[3,8,1,1]{2,1,0,3:T(8,128)S(1)}, f32[3,8,1,1]{2,1,0,3:T(8,128)S(1)}, u32[]{:S(2)}, u32[]{:S(2)}) collective-permute-start(f32[3,8,1,1]{2,1,0,3:T(8,128)S(1)} %get-tuple-element.263), channel_id=1, source_target_pairs={{1,0},{2,1},{3,2},{5,4},{6,5},{7,6},{9,8},{10,9},{11,10},{13,12},{... | collective-permute-start | bytes 296 | tf_op jit(solution)/shard_map/ppermute | solution.py:21
  21.4 9.6 %collective-permute-start.4 = (f32[3,8,1,1]{2,1,0,3:T(8,128)S(1)}, f32[3,8,1,1]{2,1,0,3:T(8,128)S(1)}, u32[]{:S(2)}, u32[]{:S(2)}) collective-permute-start(f32[3,8,1,1]{2,1,0,3:T(8,128)S(1)} %get-tuple-element.262), channel_id=1, source_target_pairs={{0,1},{1,2},{2,3},{4,5},{5,6},{6,7},{8,9},{9,10},{10,11},{12,13},{... | collective-permute-start | bytes 296 | tf_op jit(solution)/shard_map/ppermute | solution.py:19
  26.0 0.7 copy-start.6
  28.3 0.7 copy-start.8
  28.9 0.7 copy-start.7
  31.1 4.3 %collective-permute-start.7 = (f32[3,1,8,1]{2,1,0,3:T(1,128)S(1)}, f32[3,1,8,1]{2,1,0,3:T(1,128)S(1)}, u32[]{:S(2)}, u32[]{:S(2)}) collective-permute-start(f32[3,1,8,1]{2,1,0,3:T(1,128)S(1)} %get-tuple-element.261), channel_id=1, source_target_pairs={{4,0},{8,4},{12,8},{5,1},{9,5},{13,9},{6,2},{10,6},{14,10},{7,3},{... | collective-permute-start | bytes 296 | tf_op jit(solution)/shard_map/ppermute | solution.py:21
  32.4 3.8 %collective-permute-start.6 = (f32[3,1,8,1]{2,1,0,3:T(1,128)S(1)}, f32[3,1,8,1]{2,1,0,3:T(1,128)S(1)}, u32[]{:S(2)}, u32[]{:S(2)}) collective-permute-start(f32[3,1,8,1]{2,1,0,3:T(1,128)S(1)} %get-tuple-element.260), channel_id=1, source_target_pairs={{0,4},{4,8},{8,12},{1,5},{5,9},{9,13},{2,6},{6,10},{10,14},{3,7},{... | collective-permute-start | bytes 296 | tf_op jit(solution)/shard_map/ppermute | solution.py:19
  37.2 7.0 %all-to-all-start.2 = ((f32[6,3,8,1]{2,3,1,0:T(1,128)}), f32[6,3,8,1]{2,3,1,0:T(1,128)S(1)}, u32[]{:S(2)}, u32[]{:S(2)}) async-start(f32[6,3,8,1]{2,3,1,0:T(1,128)} %broadcast_multiply_fusion.7), calls=%async_computation.2 | async-start | bytes 18432 | tf_op jit(solution)/shard_map/all_to_all | solution.py:214
  44.3 7.0 %all-to-all-start.3 = ((f32[6,3,8,1]{2,3,1,0:T(1,128)}), f32[6,3,8,1]{2,3,1,0:T(1,128)S(1)}, u32[]{:S(2)}, u32[]{:S(2)}) async-start(f32[6,3,8,1]{2,3,1,0:T(1,128)} %broadcast_multiply_fusion.6), calls=%async_computation.3 | async-start | bytes 18432 | tf_op jit(solution)/shard_map/all_to_all | solution.py:215
  52.8 17.7 %collective-permute-start.3 = (f32[3,1,8,192]{3,2,1,0:T(8,128)S(1)}, f32[3,1,8,192]{3,2,1,0:T(8,128)S(1)}, u32[]{:S(2)}, u32[]{:S(2)}) collective-permute-start(f32[3,1,8,192]{3,2,1,0:T(8,128)S(1)} %slice.905), channel_id=1, source_target_pairs={{4,0},{8,4},{12,8},{5,1},{9,5},{13,9},{6,2},{10,6},{14,10},{7,3},{... | collective-permute-start | bytes 55304 | tf_op jit(solution)/shard_map/ppermute | solution.py:21
  54.1 16.4 %collective-permute-start.2 = (f32[3,1,8,192]{3,2,0,1:T(8,128)S(1)}, f32[3,1,8,192]{3,2,0,1:T(8,128)S(1)}, u32[]{:S(2)}, u32[]{:S(2)}) collective-permute-start(f32[3,1,8,192]{3,2,0,1:T(8,128)S(1)} %slice.904), channel_id=1, source_target_pairs={{0,4},{4,8},{8,12},{1,5},{5,9},{9,13},{2,6},{6,10},{10,14},{3,7},{... | collective-permute-start | bytes 55304 | tf_op jit(solution)/shard_map/ppermute | solution.py:19
  71.4 8.0 %all-to-all-start = ((f32[6,3,8,192]{3,2,1,0:T(8,128)}), f32[6,3,8,192]{3,2,1,0:T(8,128)S(1)}, u32[]{:S(2)}, u32[]{:S(2)}) async-start(f32[6,3,8,192]{3,2,1,0:T(8,128)} %broadcast_multiply_fusion.5), calls=%async_computation | async-start | bytes 294912 | tf_op jit(solution)/shard_map/all_to_all | solution.py:214
  79.4 8.0 %all-to-all-start.1 = ((f32[6,3,8,192]{3,2,1,0:T(8,128)}), f32[6,3,8,192]{3,2,1,0:T(8,128)S(1)}, u32[]{:S(2)}, u32[]{:S(2)}) async-start(f32[6,3,8,192]{3,2,1,0:T(8,128)} %broadcast_multiply_fusion.4), calls=%async_computation.1 | async-start | bytes 294912 | tf_op jit(solution)/shard_map/all_to_all | solution.py:215
  82.8 41.7 %all-reduce.13.cloned.1.call-start = ((), (), s32[]{:S(2)}) async-start(), calls=%async_computation.14 | async-start | bytes 393216
  89.7 36.3 %reduce-scatter.7.cloned.1.call-start = ((), (), s32[]{:S(2)}) async-start(), calls=%async_computation.11 | async-start | bytes 245760 | tf_op jit(solution)/shard_map/reduce_scatter | solution.py:240
  160.6 5.9 %collective-permute-start.9 = (f32[3,8,1,192]{3,2,0,1:T(1,128)S(1)}, f32[3,8,1,192]{3,2,0,1:T(1,128)S(1)}, u32[]{:S(2)}, u32[]{:S(2)}) collective-permute-start(f32[3,8,1,192]{3,2,0,1:T(1,128)S(1)} %get-tuple-element.231), channel_id=1, source_target_pairs={{1,0},{2,1},{3,2},{5,4},{6,5},{7,6},{9,8},{10,9},{11,10},{13,12},{... | collective-permute-start | bytes 55304 | tf_op jit(solution)/shard_map/ppermute | solution.py:21
  161.9 6.1 %collective-permute-start.8 = (f32[3,8,1,192]{3,2,0,1:T(1,128)S(1)}, f32[3,8,1,192]{3,2,0,1:T(1,128)S(1)}, u32[]{:S(2)}, u32[]{:S(2)}) collective-permute-start(f32[3,8,1,192]{3,2,0,1:T(1,128)S(1)} %get-tuple-element.230), channel_id=1, source_target_pairs={{0,1},{1,2},{2,3},{4,5},{5,6},{6,7},{8,9},{9,10},{10,11},{12,13},{... | collective-permute-start | bytes 55304 | tf_op jit(solution)/shard_map/ppermute | solution.py:19
  168.0 4.5 %collective-permute-start.11 = (f32[3,1,8,192]{3,2,0,1:T(8,128)S(1)}, f32[3,1,8,192]{3,2,0,1:T(8,128)S(1)}, u32[]{:S(2)}, u32[]{:S(2)}) collective-permute-start(f32[3,1,8,192]{3,2,0,1:T(8,128)S(1)} %get-tuple-element.229), channel_id=1, source_target_pairs={{4,0},{8,4},{12,8},{5,1},{9,5},{13,9},{6,2},{10,6},{14,10},{7,3},{... | collective-permute-start | bytes 55304 | tf_op jit(solution)/shard_map/ppermute | solution.py:21
  169.3 3.9 %collective-permute-start.10 = (f32[3,1,8,192]{3,2,0,1:T(8,128)S(1)}, f32[3,1,8,192]{3,2,0,1:T(8,128)S(1)}, u32[]{:S(2)}, u32[]{:S(2)}) collective-permute-start(f32[3,1,8,192]{3,2,0,1:T(8,128)S(1)} %get-tuple-element.228), channel_id=1, source_target_pairs={{0,4},{4,8},{8,12},{1,5},{5,9},{9,13},{2,6},{6,10},{10,14},{3,7},{... | collective-permute-start | bytes 55304 | tf_op jit(solution)/shard_map/ppermute | solution.py:19
  174.1 8.2 %all-to-all-start.4 = ((f32[6,3,8,192]{3,2,1,0:T(8,128)}), f32[6,3,8,192]{3,2,1,0:T(8,128)S(1)}, u32[]{:S(2)}, u32[]{:S(2)}) async-start(f32[6,3,8,192]{3,2,1,0:T(8,128)} %broadcast_multiply_fusion.3), calls=%async_computation.4 | async-start | bytes 294912 | tf_op jit(solution)/shard_map/all_to_all | solution.py:214
  182.3 8.2 %all-to-all-start.5 = ((f32[6,3,8,192]{3,2,1,0:T(8,128)}), f32[6,3,8,192]{3,2,1,0:T(8,128)S(1)}, u32[]{:S(2)}, u32[]{:S(2)}) async-start(f32[6,3,8,192]{3,2,1,0:T(8,128)} %broadcast_multiply_fusion.2), calls=%async_computation.5 | async-start | bytes 294912 | tf_op jit(solution)/shard_map/all_to_all | solution.py:215
  185.7 43.1 %all-reduce.15.cloned.1.call-start = ((), (), s32[]{:S(2)}) async-start(), calls=%async_computation.15 | async-start | bytes 393216
  192.8 48.1 %reduce-scatter.9.cloned.1.call-start = ((), (), s32[]{:S(2)}) async-start(), calls=%async_computation.12 | async-start | bytes 245760 | tf_op jit(solution)/shard_map/reduce_scatter | solution.py:240
  263.2 5.9 %collective-permute-start.13 = (f32[3,8,1,192]{3,2,0,1:T(1,128)S(1)}, f32[3,8,1,192]{3,2,0,1:T(1,128)S(1)}, u32[]{:S(2)}, u32[]{:S(2)}) collective-permute-start(f32[3,8,1,192]{3,2,0,1:T(1,128)S(1)} %get-tuple-element.227), channel_id=1, source_target_pairs={{1,0},{2,1},{3,2},{5,4},{6,5},{7,6},{9,8},{10,9},{11,10},{13,12},{... | collective-permute-start | bytes 55304 | tf_op jit(solution)/shard_map/ppermute | solution.py:21
  264.5 6.1 %collective-permute-start.12 = (f32[3,8,1,192]{3,2,0,1:T(1,128)S(1)}, f32[3,8,1,192]{3,2,0,1:T(1,128)S(1)}, u32[]{:S(2)}, u32[]{:S(2)}) collective-permute-start(f32[3,8,1,192]{3,2,0,1:T(1,128)S(1)} %get-tuple-element.226), channel_id=1, source_target_pairs={{0,1},{1,2},{2,3},{4,5},{5,6},{6,7},{8,9},{9,10},{10,11},{12,13},{... | collective-permute-start | bytes 55304 | tf_op jit(solution)/shard_map/ppermute | solution.py:19
  270.6 4.3 %collective-permute-start.15 = (f32[3,1,8,192]{3,2,0,1:T(8,128)S(1)}, f32[3,1,8,192]{3,2,0,1:T(8,128)S(1)}, u32[]{:S(2)}, u32[]{:S(2)}) collective-permute-start(f32[3,1,8,192]{3,2,0,1:T(8,128)S(1)} %get-tuple-element.225), channel_id=1, source_target_pairs={{4,0},{8,4},{12,8},{5,1},{9,5},{13,9},{6,2},{10,6},{14,10},{7,3},{... | collective-permute-start | bytes 55304 | tf_op jit(solution)/shard_map/ppermute | solution.py:21
  271.9 3.9 %collective-permute-start.14 = (f32[3,1,8,192]{3,2,0,1:T(8,128)S(1)}, f32[3,1,8,192]{3,2,0,1:T(8,128)S(1)}, u32[]{:S(2)}, u32[]{:S(2)}) collective-permute-start(f32[3,1,8,192]{3,2,0,1:T(8,128)S(1)} %get-tuple-element.224), channel_id=1, source_target_pairs={{0,4},{4,8},{8,12},{1,5},{5,9},{9,13},{2,6},{6,10},{10,14},{3,7},{... | collective-permute-start | bytes 55304 | tf_op jit(solution)/shard_map/ppermute | solution.py:19
  276.7 8.2 %all-to-all-start.6 = ((f32[6,3,8,192]{3,2,1,0:T(8,128)}), f32[6,3,8,192]{3,2,1,0:T(8,128)S(1)}, u32[]{:S(2)}, u32[]{:S(2)}) async-start(f32[6,3,8,192]{3,2,1,0:T(8,128)} %broadcast_multiply_fusion.1), calls=%async_computation.6 | async-start | bytes 294912 | tf_op jit(solution)/shard_map/all_to_all | solution.py:214
  284.9 8.2 %all-to-all-start.7 = ((f32[6,3,8,192]{3,2,1,0:T(8,128)}), f32[6,3,8,192]{3,2,1,0:T(8,128)S(1)}, u32[]{:S(2)}, u32[]{:S(2)}) async-start(f32[6,3,8,192]{3,2,1,0:T(8,128)} %broadcast_multiply_fusion), calls=%async_computation.7 | async-start | bytes 294912 | tf_op jit(solution)/shard_map/all_to_all | solution.py:215
  288.4 43.0 %all-reduce.17.cloned.1.call-start = ((), (), s32[]{:S(2)}) async-start(), calls=%async_computation.16 | async-start | bytes 393216
  295.4 48.0 %reduce-scatter.11.cloned.1.call-start = ((), (), s32[]{:S(2)}) async-start(), calls=%async_computation.13 | async-start | bytes 245760 | tf_op jit(solution)/shard_map/reduce_scatter | solution.py:240
Sparse Core Ops, SparseCore 0:
  89.8 34.6 all-reduce.12
  192.9 35.8 all-reduce.14
  295.5 35.7 all-reduce.16
Sparse Core Ops, SparseCore 1:
  92.6 19.4 reduce-scatter.6
  195.7 20.6 reduce-scatter.8
  298.3 20.6 reduce-scatter.10
where the time goes:
time: 373 us; the launch traced here: 371 us
  waiting for transfers between devices  139 us (37%)
  blocking collectives  99.7 us (27%)
  starting transfers between devices  69.1 us (19%)
  local copies, waits for them, and re-layouts  26.4 us (7%)
  between operations  16.4 us (4%)
  other arithmetic  12.6 us (3%)
  matrix products  7.16 us (2%)
    unnamed x9, waiting for transfers between devices  103 us
    psum x3, blocking collectives, assemble(): tall_whole = lax.psum(tall_lines, 'fx')  54.8 us
    psum x3, blocking collectives, assemble(): flat_whole = lax.psum(flat_lines, 'fy')  31.7 us
    ppermute x8, starting transfers between devices, padded(): lax.ppermute(tail, axis, [(i, (i + 1) % count) for i in range(ends)])  31.5 us
    all_to_all x4, waiting for transfers between devices, assemble(): lax.all_to_all(send_tall, 'face', split_axis=0, concat_axis=1, tiled=True)  16.2 us
    all_to_all x4, waiting for transfers between devices, assemble(): lax.all_to_all(send_flat, 'face', split_axis=0, concat_axis=1, tiled=True)  14.9 us
    all_to_all x4, starting transfers between devices, assemble(): lax.all_to_all(send_flat, 'face', split_axis=0, concat_axis=1, tiled=True)  13.5 us
    all_to_all x4, starting transfers between devices, assemble(): lax.all_to_all(send_tall, 'face', split_axis=0, concat_axis=1, tiled=True)  13.5 us
  transfers between devices with their start and end apart: 30, of which 16 were waited for; matrix products, arithmetic and copies ran while one was open for 5% of the time, Pallas kernels for 0%

commit v1 on v0

--- a/solution.py
+++ b/solution.py
@@ -234,7 +234,7 @@
     flat_lines = flat_lines.reshape(face_local, 2, lax.axis_size("fx"), col_count, chan_count)
     tall_lines = jnp.stack([rim_strips[:, 1], rim_strips[:, 3, ::-1]], axis=1)
     tall_lines = tall_lines.reshape(face_local, 2, lax.axis_size("fy"), row_count, chan_count)
-    flat_whole = lax.psum(flat_lines, "fy")
+    flat_whole = jnp.sum(lax.all_gather(flat_lines, "fy"), axis=0)
     tall_whole = lax.psum(tall_lines, "fx")
     flat_block = lax.psum_scatter(flat_whole, "fx", scatter_dimension=2, tiled=True)
     tall_block = lax.psum_scatter(tall_whole, "fy", scatter_dimension=2, tiled=True)

time: 373 us -> 374 us (level)
  starting transfers between devices: 69.1 us -> 55 us
  waiting for transfers between devices: 139 us -> 150 us
  other arithmetic: 12.6 us -> 21.6 us
  local copies, waits for them, and re-layouts: 26.4 us -> 21.6 us
    all_gather x0 -> x4, blocking collectives: none -> 33.1 us  [assemble(): flat_whole = jnp.sum(lax.all_gather(flat_lines, 'fy'), axis=0)]
    psum x3 -> x0, blocking collectives: 31.7 us -> none  [assemble(): flat_whole = lax.psum(flat_lines, 'fy')]
    ppermute x8, waiting for transfers between devices: 0.02 us -> 20.4 us  [padded(): lax.ppermute(head, axis, [((i + 1) % count, i) for i in range(ends)])]
    ppermute x8, starting transfers between devices: 31.5 us -> 17.2 us  [padded(): lax.ppermute(tail, axis, [(i, (i + 1) % count) for i in range(ends)])]
    ppermute x8, waiting for transfers between devices: 5.24 us -> 0.24 us  [padded(): lax.ppermute(tail, axis, [(i, (i + 1) % count) for i in range(ends)])]
    unnamed x33 -> x29, local copies, waits for them, and re-layouts: 10.3 us -> 5.38 us
    unnamed x9, waiting for transfers between devices: 103 us -> 98.3 us
    scatter-add x3, other arithmetic: 0.03 us -> 4.15 us  [assemble(): result = summed.at[:, 0].add(jnp.where(on_south, flat_add, 0.0))]
  transfers between devices with their start and end apart: 30 -> 30, of which waited for: 16 -> 18; matrix products, arithmetic and copies ran while one was open for 5% -> 6% of each run, Pallas kernels for 0% -> 0%
where the time goes in v1:
time: 374 us; the launch traced here: 372 us
  waiting for transfers between devices  150 us (40%)
  blocking collectives  99.8 us (27%)
  starting transfers between devices  55 us (15%)
  local copies, waits for them, and re-layouts  21.6 us (6%)
  other arithmetic  21.6 us (6%)
  between operations  16.4 us (4%)
  matrix products  7.15 us (2%)
    unnamed x9, waiting for transfers between devices  98.3 us
    psum x3, blocking collectives, assemble(): tall_whole = lax.psum(tall_lines, 'fx')  54.8 us
    all_gather x4, blocking collectives, assemble(): flat_whole = jnp.sum(lax.all_gather(flat_lines, 'fy'), axis=0)  33.1 us
    ppermute x8, waiting for transfers between devices, padded(): lax.ppermute(head, axis, [((i + 1) % count, i) for i in range(ends)])  20.4 us
    ppermute x8, starting transfers between devices, padded(): lax.ppermute(tail, axis, [(i, (i + 1) % count) for i in range(ends)])  17.2 us
    all_to_all x4, waiting for transfers between devices, assemble(): lax.all_to_all(send_flat, 'face', split_axis=0, concat_axis=1, tiled=True)  16.3 us
    all_to_all x4, waiting for transfers between devices, assemble(): lax.all_to_all(send_tall, 'face', split_axis=0, concat_axis=1, tiled=True)  15 us
    all_to_all x4, starting transfers between devices, assemble(): lax.all_to_all(send_flat, 'face', split_axis=0, concat_axis=1, tiled=True)  13.5 us
  transfers between devices with their start and end apart: 30, of which 18 were waited for; matrix products, arithmetic and copies ran while one was open for 6% of the time, Pallas kernels for 0%

profile of v1, /device:TPU:0, one launch (start us, length us, event | category | flops | bytes accessed | tf_op | source)
XLA Modules:
  0.0 372.0 jit_solution(10273628878758850990)
XLA Ops:
  7.4 0.8 fusion.161
  8.1 1.0 slice.770
  13.1 5.0 %collective-permute-start = (f32[3,8,1,192]{3,2,0,1:T(1,128)S(1)}, f32[3,8,1,192]{3,2,0,1:T(1,128)S(1)}, u32[]{:S(2)}, u32[]{:S(2)}) collective-permute-start(f32[3,8,1,192]{3,2,0,1:T(1,128)S(1)} %slice.902), channel_id=1, source_target_pairs={{0,1},{1,2},{2,3},{4,5},{5,6},{6,7},{8,9},{9,10},{10,11},{12,13},{... | collective-permute-start | bytes 55304 | tf_op jit(solution)/shard_map/ppermute | solution.py:19
  18.1 1.3 collective-permute-start.1
  19.5 4.5 %collective-permute-start.4 = (f32[3,8,1,1]{2,1,0,3:T(8,128)S(1)}, f32[3,8,1,1]{2,1,0,3:T(8,128)S(1)}, u32[]{:S(2)}, u32[]{:S(2)}) collective-permute-start(f32[3,8,1,1]{2,1,0,3:T(8,128)S(1)} %get-tuple-element.262), channel_id=1, source_target_pairs={{0,1},{1,2},{2,3},{4,5},{5,6},{6,7},{8,9},{9,10},{10,11},{12,13},{... | collective-permute-start | bytes 296 | tf_op jit(solution)/shard_map/ppermute | solution.py:19
  24.0 1.3 collective-permute-start.5
  30.5 1.3 collective-permute-start.6
  31.8 1.3 collective-permute-start.7
  33.1 3.5 collective-permute-done.7
  37.5 3.2 all-to-all-start.2
  41.4 3.1 all-to-all-done.2
  44.6 3.2 all-to-all-start.3
  48.0 3.7 all-to-all-done.3
  52.9 5.5 %all_gather.13 = f32[4,3,2,4,8,1]{4,3,5,2,1,0:T(4,128)S(1)} all-gather(f32[1,3,2,4,8,1]{4,3,5,2,1,0:T(4,128)S(1)} %bitcast.363), channel_id=1, replica_groups=mesh['face'=2,'fy'=4,'fx'=4] {'fy'}, dimensions={0}, use_global_device_ids=true | all-gather | bytes 3840 | tf_op jit(solution)/shard_map/all_gather | solution.py:237
  58.6 11.9 %all-reduce.4 = f32[3,2,4,8,1]{3,1,4,0,2:T(2,128)S(1)} all-reduce(f32[3,2,4,8,1]{3,1,4,0,2:T(2,128)S(1)} %copy.276), channel_id=5, replica_groups=mesh['face'=2,'fy'=4,'fx'=4] {'fy'}, use_global_device_ids=true, to_apply=%region_7.8.clone | all-reduce | flops 192 | bytes 1536
  70.7 1.3 collective-permute-start.2
  72.0 1.3 collective-permute-start.3
  74.0 1.7 collective-permute-done.3
  76.6 3.4 all-to-all-start.1
  80.1 0.7 broadcast_multiply_fusion.5
  80.8 3.8 %all-to-all-done.1 = f32[6,3,8,192]{3,2,1,0:T(8,128)S(1)} async-done(((f32[6,3,8,192]{3,2,1,0:T(8,128)}), f32[6,3,8,192]{3,2,1,0:T(8,128)S(1)}, u32[]{:S(2)}, u32[]{:S(2)}) %all-to-all-start.1) | async-done | bytes 110624 | tf_op jit(solution)/shard_map/all_to_all | solution.py:215
  84.6 3.4 all-to-all-start
  88.5 4.4 %all-to-all-done = f32[6,3,8,192]{3,2,1,0:T(8,128)S(1)} async-done(((f32[6,3,8,192]{3,2,1,0:T(8,128)}), f32[6,3,8,192]{3,2,1,0:T(8,128)S(1)}, u32[]{:S(2)}, u32[]{:S(2)}) %all-to-all-start) | async-done | bytes 110624 | tf_op jit(solution)/shard_map/all_to_all | solution.py:214
  94.5 9.2 %all_gather.12 = f32[4,3,2,4,8,192]{5,4,3,2,1,0:T(8,128)S(1)} all-gather(f32[1,3,2,4,8,192]{5,4,3,2,1,0:T(8,128)S(1)} %copy.258), channel_id=1, replica_groups=mesh['face'=2,'fy'=4,'fx'=4] {'fy'}, dimensions={0}, use_global_device_ids=true | all-gather | bytes 737280 | tf_op jit(solution)/shard_map/all_gather | solution.py:237
  105.6 34.9 %all-reduce.12.cloned.1.call-done = f32[3,2,4,8,192]{4,3,0,2,1:T(8,128)} async-done(((f32[3,2,4,8,192]{4,3,0,2,1:T(8,128)}), f32[3,2,4,8,192]{4,3,0,2,1:T(8,128)}) %all-reduce.12.cloned.1.call-update) | async-done | bytes 147472
  140.5 1.4 bitcast_dynamic-update-slice_fusion
  141.9 1.4 fusion.100
  143.3 0.8 copy.267
  144.1 18.5 %all-reduce.7 = (f32[3,2,1,8,192]{4,1,3,2,0:T(2,128)S(1)}, f32[3,2,4,8,1]{3,1,4,0,2:T(2,128)S(1)}, f32[3,2,1,8,1]{3,1,4,0,2:T(2,128)S(1)}) all-reduce(f32[3,2,1,8,192]{4,1,3,2,0:T(2,128)S(1)} %copy.267, f32[3,2,4,8,1]{3,1,4,0,2:T(2,128)S(1)} %copy.273, ...), channel_id=1, replica_groups=mesh['face'=2,'fy'=4,'fx'=4] {'fx'}, use_global_device_ids=true, to_apply=%region_2.3 | all-reduce | flops 9456 | bytes 75648 | tf_op jit(solution)/shard_map/psum | solution.py:238
  167.2 1.3 collective-permute-start.8
  168.5 1.5 collective-permute-start.9
  170.0 4.2 %collective-permute-done.9 = f32[3,8,1,192]{3,2,0,1:T(1,128)S(1)} collective-permute-done((f32[3,8,1,192]{3,2,0,1:T(1,128)S(1)}, f32[3,8,1,192]{3,2,0,1:T(1,128)S(1)}, u32[]{:S(2)}, u32[]{:S(2)}) %collective-permute-start.9) | collective-permute-done | bytes 18464 | tf_op jit(solution)/shard_map/ppermute | solution.py:21
  174.3 1.3 collective-permute-start.10
  175.6 1.3 collective-permute-start.11
  176.9 3.4 collective-permute-done.11
  181.3 3.4 all-to-all-start.5
  184.7 0.7 broadcast_multiply_fusion.3
  185.4 3.8 %all-to-all-done.5 = f32[6,3,8,192]{3,2,1,0:T(8,128)S(1)} async-done(((f32[6,3,8,192]{3,2,1,0:T(8,128)}), f32[6,3,8,192]{3,2,1,0:T(8,128)S(1)}, u32[]{:S(2)}, u32[]{:S(2)}) %all-to-all-start.5) | async-done | bytes 110624 | tf_op jit(solution)/shard_map/all_to_all | solution.py:215
  189.2 3.4 all-to-all-start.4
  193.2 4.4 %all-to-all-done.4 = f32[6,3,8,192]{3,2,1,0:T(8,128)S(1)} async-done(((f32[6,3,8,192]{3,2,1,0:T(8,128)}), f32[6,3,8,192]{3,2,1,0:T(8,128)S(1)}, u32[]{:S(2)}, u32[]{:S(2)}) %all-to-all-start.4) | async-done | bytes 110624 | tf_op jit(solution)/shard_map/all_to_all | solution.py:214
  199.2 9.2 %all_gather.14 = f32[4,3,2,4,8,192]{5,4,3,2,1,0:T(8,128)S(1)} all-gather(f32[1,3,2,4,8,192]{5,4,3,2,1,0:T(8,128)S(1)} %copy.300), channel_id=1, replica_groups=mesh['face'=2,'fy'=4,'fx'=4] {'fy'}, dimensions={0}, use_global_device_ids=true | all-gather | bytes 737280 | tf_op jit(solution)/shard_map/all_gather | solution.py:237
  210.2 31.7 %all-reduce.14.cloned.1.call-done = f32[3,2,4,8,192]{4,3,0,2,1:T(8,128)} async-done(((f32[3,2,4,8,192]{4,3,0,2,1:T(8,128)}), f32[3,2,4,8,192]{4,3,0,2,1:T(8,128)}) %all-reduce.14.cloned.1.call-update) | async-done | bytes 147472
  241.9 1.4 fusion.104
  243.3 1.4 fusion.96
  244.7 0.8 copy.308
  245.5 18.2 %psum.34 = f32[3,2,1,8,192]{4,1,3,2,0:T(2,128)S(1)} all-reduce(f32[3,2,1,8,192]{4,1,3,2,0:T(2,128)S(1)} %copy.308), channel_id=1, replica_groups=mesh['face'=2,'fy'=4,'fx'=4] {'fx'}, use_global_device_ids=true, to_apply=%region_10.11 | all-reduce | flops 9216 | bytes 73728 | tf_op jit(solution)/shard_map/psum | solution.py:238
  267.0 1.3 collective-permute-start.12
  268.3 1.3 collective-permute-start.13
  269.8 4.2 %collective-permute-done.13 = f32[3,8,1,192]{3,2,0,1:T(1,128)S(1)} collective-permute-done((f32[3,8,1,192]{3,2,0,1:T(1,128)S(1)}, f32[3,8,1,192]{3,2,0,1:T(1,128)S(1)}, u32[]{:S(2)}, u32[]{:S(2)}) %collective-permute-start.13) | collective-permute-done | bytes 18464 | tf_op jit(solution)/shard_map/ppermute | solution.py:21
  274.1 1.3 collective-permute-start.14
  275.4 1.3 collective-permute-start.15
  276.7 3.4 collective-permute-done.15
  281.0 3.4 all-to-all-start.7
  284.5 0.7 broadcast_multiply_fusion.1
  285.2 3.8 %all-to-all-done.7 = f32[6,3,8,192]{3,2,1,0:T(8,128)S(1)} async-done(((f32[6,3,8,192]{3,2,1,0:T(8,128)}), f32[6,3,8,192]{3,2,1,0:T(8,128)S(1)}, u32[]{:S(2)}, u32[]{:S(2)}) %all-to-all-start.7) | async-done | bytes 110624 | tf_op jit(solution)/shard_map/all_to_all | solution.py:215
  289.0 3.4 all-to-all-start.6
  292.9 4.4 %all-to-all-done.6 = f32[6,3,8,192]{3,2,1,0:T(8,128)S(1)} async-done(((f32[6,3,8,192]{3,2,1,0:T(8,128)}), f32[6,3,8,192]{3,2,1,0:T(8,128)S(1)}, u32[]{:S(2)}, u32[]{:S(2)}) %all-to-all-start.6) | async-done | bytes 110624 | tf_op jit(solution)/shard_map/all_to_all | solution.py:214
  298.9 9.2 %all_gather.15 = f32[4,3,2,4,8,192]{5,4,3,2,1,0:T(8,128)S(1)} all-gather(f32[1,3,2,4,8,192]{5,4,3,2,1,0:T(8,128)S(1)} %copy.320), channel_id=1, replica_groups=mesh['face'=2,'fy'=4,'fx'=4] {'fy'}, dimensions={0}, use_global_device_ids=true | all-gather | bytes 737280 | tf_op jit(solution)/shard_map/all_gather | solution.py:237
  310.0 31.6 %all-reduce.16.cloned.1.call-done = f32[3,2,4,8,192]{4,3,0,2,1:T(8,128)} async-done(((f32[3,2,4,8,192]{4,3,0,2,1:T(8,128)}), f32[3,2,4,8,192]{4,3,0,2,1:T(8,128)}) %all-reduce.16.cloned.1.call-update) | async-done | bytes 147472
  341.6 1.4 fusion.103
  343.0 1.4 fusion.93
  344.4 0.8 copy.326
  345.3 18.2 %psum.35 = f32[3,2,1,8,192]{4,1,3,2,0:T(2,128)S(1)} all-reduce(f32[3,2,1,8,192]{4,1,3,2,0:T(2,128)S(1)} %copy.326), channel_id=1, replica_groups=mesh['face'=2,'fy'=4,'fx'=4] {'fx'}, use_global_device_ids=true, to_apply=%region_14.15 | all-reduce | flops 9216 | bytes 73728 | tf_op jit(solution)/shard_map/psum | solution.py:238
  363.8 0.8 multiply_subtract_fusion
  (256 shorter events, 35.3 us)
Async XLA Ops:
  7.4 19.0 %copy-start = (s32[6,4]{0,1:T(4,128)S(1)}, s32[6,4]{0,1:T(4,128)}, u32[]{:S(2)}) copy-start(s32[6,4]{0,1:T(4,128)} %param.55) | copy-start | bytes 292
  7.4 1.8 copy-start.1
  8.1 1.0 copy-start.3
  9.5 0.7 copy-start.4
  11.2 0.7 copy-start.9
  11.2 0.7 copy-start.2
  12.0 0.7 copy-start.5
  13.1 57.4 %collective-permute-start = (f32[3,8,1,192]{3,2,0,1:T(1,128)S(1)}, f32[3,8,1,192]{3,2,0,1:T(1,128)S(1)}, u32[]{:S(2)}, u32[]{:S(2)}) collective-permute-start(f32[3,8,1,192]{3,2,0,1:T(1,128)S(1)} %slice.902), channel_id=1, source_target_pairs={{0,1},{1,2},{2,3},{4,5},{5,6},{6,7},{8,9},{9,10},{10,11},{12,13},{... | collective-permute-start | bytes 55304 | tf_op jit(solution)/shard_map/ppermute | solution.py:19
  18.1 52.4 %collective-permute-start.1 = (f32[3,8,1,192]{3,2,1,0:T(1,128)S(1)}, f32[3,8,1,192]{3,2,1,0:T(1,128)S(1)}, u32[]{:S(2)}, u32[]{:S(2)}) collective-permute-start(f32[3,8,1,192]{3,2,1,0:T(1,128)S(1)} %slice.903), channel_id=1, source_target_pairs={{1,0},{2,1},{3,2},{5,4},{6,5},{7,6},{9,8},{10,9},{11,10},{13,12},{... | collective-permute-start | bytes 55304 | tf_op jit(solution)/shard_map/ppermute | solution.py:21
  19.5 10.9 %collective-permute-start.4 = (f32[3,8,1,1]{2,1,0,3:T(8,128)S(1)}, f32[3,8,1,1]{2,1,0,3:T(8,128)S(1)}, u32[]{:S(2)}, u32[]{:S(2)}) collective-permute-start(f32[3,8,1,1]{2,1,0,3:T(8,128)S(1)} %get-tuple-element.262), channel_id=1, source_target_pairs={{0,1},{1,2},{2,3},{4,5},{5,6},{6,7},{8,9},{9,10},{10,11},{12,13},{... | collective-permute-start | bytes 296 | tf_op jit(solution)/shard_map/ppermute | solution.py:19
  24.0 6.4 %collective-permute-start.5 = (f32[3,8,1,1]{2,1,0,3:T(8,128)S(1)}, f32[3,8,1,1]{2,1,0,3:T(8,128)S(1)}, u32[]{:S(2)}, u32[]{:S(2)}) collective-permute-start(f32[3,8,1,1]{2,1,0,3:T(8,128)S(1)} %get-tuple-element.263), channel_id=1, source_target_pairs={{1,0},{2,1},{3,2},{5,4},{6,5},{7,6},{9,8},{10,9},{11,10},{13,12},{... | collective-permute-start | bytes 296 | tf_op jit(solution)/shard_map/ppermute | solution.py:21
  25.4 0.7 copy-start.6
  27.6 0.7 copy-start.8
  28.3 0.7 copy-start.7
  30.5 2.6 collective-permute-start.6
  31.8 4.8 %collective-permute-start.7 = (f32[3,1,8,1]{2,1,0,3:T(1,128)S(1)}, f32[3,1,8,1]{2,1,0,3:T(1,128)S(1)}, u32[]{:S(2)}, u32[]{:S(2)}) collective-permute-start(f32[3,1,8,1]{2,1,0,3:T(1,128)S(1)} %get-tuple-element.261), channel_id=1, source_target_pairs={{4,0},{8,4},{12,8},{5,1},{9,5},{13,9},{6,2},{10,6},{14,10},{7,3},{... | collective-permute-start | bytes 296 | tf_op jit(solution)/shard_map/ppermute | solution.py:21
  37.5 7.0 %all-to-all-start.2 = ((f32[6,3,8,1]{2,3,1,0:T(1,128)}), f32[6,3,8,1]{2,3,1,0:T(1,128)S(1)}, u32[]{:S(2)}, u32[]{:S(2)}) async-start(f32[6,3,8,1]{2,3,1,0:T(1,128)} %broadcast_multiply_fusion.7), calls=%async_computation.2 | async-start | bytes 18432 | tf_op jit(solution)/shard_map/all_to_all | solution.py:214
  44.6 7.0 %all-to-all-start.3 = ((f32[6,3,8,1]{2,3,1,0:T(1,128)}), f32[6,3,8,1]{2,3,1,0:T(1,128)S(1)}, u32[]{:S(2)}, u32[]{:S(2)}) async-start(f32[6,3,8,1]{2,3,1,0:T(1,128)} %broadcast_multiply_fusion.6), calls=%async_computation.3 | async-start | bytes 18432 | tf_op jit(solution)/shard_map/all_to_all | solution.py:215
  70.7 3.3 collective-permute-start.2
  72.0 3.7 %collective-permute-start.3 = (f32[3,1,8,192]{3,2,1,0:T(8,128)S(1)}, f32[3,1,8,192]{3,2,1,0:T(8,128)S(1)}, u32[]{:S(2)}, u32[]{:S(2)}) collective-permute-start(f32[3,1,8,192]{3,2,1,0:T(8,128)S(1)} %slice.905), channel_id=1, source_target_pairs={{4,0},{8,4},{12,8},{5,1},{9,5},{13,9},{6,2},{10,6},{14,10},{7,3},{... | collective-permute-start | bytes 55304 | tf_op jit(solution)/shard_map/ppermute | solution.py:21
  76.6 8.0 %all-to-all-start.1 = ((f32[6,3,8,192]{3,2,1,0:T(8,128)}), f32[6,3,8,192]{3,2,1,0:T(8,128)S(1)}, u32[]{:S(2)}, u32[]{:S(2)}) async-start(f32[6,3,8,192]{3,2,1,0:T(8,128)} %broadcast_multiply_fusion.4), calls=%async_computation.1 | async-start | bytes 294912 | tf_op jit(solution)/shard_map/all_to_all | solution.py:215
  84.6 8.3 %all-to-all-start = ((f32[6,3,8,192]{3,2,1,0:T(8,128)}), f32[6,3,8,192]{3,2,1,0:T(8,128)S(1)}, u32[]{:S(2)}, u32[]{:S(2)}) async-start(f32[6,3,8,192]{3,2,1,0:T(8,128)} %broadcast_multiply_fusion.5), calls=%async_computation | async-start | bytes 294912 | tf_op jit(solution)/shard_map/all_to_all | solution.py:214
  88.0 52.4 %all-reduce.12.cloned.1.call-start = ((), (), s32[]{:S(2)}) async-start(), calls=%async_computation.14 | async-start | bytes 393216
  104.5 38.7 %reduce-scatter.7.cloned.1.call-start = ((), (), s32[]{:S(2)}) async-start(), calls=%async_computation.11 | async-start | bytes 245760 | tf_op jit(solution)/shard_map/reduce_scatter | solution.py:240
  167.2 2.8 collective-permute-start.8
  168.5 5.7 %collective-permute-start.9 = (f32[3,8,1,192]{3,2,0,1:T(1,128)S(1)}, f32[3,8,1,192]{3,2,0,1:T(1,128)S(1)}, u32[]{:S(2)}, u32[]{:S(2)}) collective-permute-start(f32[3,8,1,192]{3,2,0,1:T(1,128)S(1)} %get-tuple-element.231), channel_id=1, source_target_pairs={{1,0},{2,1},{3,2},{5,4},{6,5},{7,6},{9,8},{10,9},{11,10},{13,12},{... | collective-permute-start | bytes 55304 | tf_op jit(solution)/shard_map/ppermute | solution.py:21
  174.3 2.6 collective-permute-start.10
  175.6 4.7 %collective-permute-start.11 = (f32[3,1,8,192]{3,2,0,1:T(8,128)S(1)}, f32[3,1,8,192]{3,2,0,1:T(8,128)S(1)}, u32[]{:S(2)}, u32[]{:S(2)}) collective-permute-start(f32[3,1,8,192]{3,2,0,1:T(8,128)S(1)} %get-tuple-element.229), channel_id=1, source_target_pairs={{4,0},{8,4},{12,8},{5,1},{9,5},{13,9},{6,2},{10,6},{14,10},{7,3},{... | collective-permute-start | bytes 55304 | tf_op jit(solution)/shard_map/ppermute | solution.py:21
  181.3 8.0 %all-to-all-start.5 = ((f32[6,3,8,192]{3,2,1,0:T(8,128)}), f32[6,3,8,192]{3,2,1,0:T(8,128)S(1)}, u32[]{:S(2)}, u32[]{:S(2)}) async-start(f32[6,3,8,192]{3,2,1,0:T(8,128)} %broadcast_multiply_fusion.2), calls=%async_computation.5 | async-start | bytes 294912 | tf_op jit(solution)/shard_map/all_to_all | solution.py:215
  189.2 8.3 %all-to-all-start.4 = ((f32[6,3,8,192]{3,2,1,0:T(8,128)}), f32[6,3,8,192]{3,2,1,0:T(8,128)S(1)}, u32[]{:S(2)}, u32[]{:S(2)}) async-start(f32[6,3,8,192]{3,2,1,0:T(8,128)} %broadcast_multiply_fusion.3), calls=%async_computation.4 | async-start | bytes 294912 | tf_op jit(solution)/shard_map/all_to_all | solution.py:214
  192.7 49.2 %all-reduce.14.cloned.1.call-start = ((), (), s32[]{:S(2)}) async-start(), calls=%async_computation.15 | async-start | bytes 393216
  209.2 35.5 %reduce-scatter.9.cloned.1.call-start = ((), (), s32[]{:S(2)}) async-start(), calls=%async_computation.12 | async-start | bytes 245760 | tf_op jit(solution)/shard_map/reduce_scatter | solution.py:240
  267.0 2.8 collective-permute-start.12
  268.3 5.7 %collective-permute-start.13 = (f32[3,8,1,192]{3,2,0,1:T(1,128)S(1)}, f32[3,8,1,192]{3,2,0,1:T(1,128)S(1)}, u32[]{:S(2)}, u32[]{:S(2)}) collective-permute-start(f32[3,8,1,192]{3,2,0,1:T(1,128)S(1)} %get-tuple-element.227), channel_id=1, source_target_pairs={{1,0},{2,1},{3,2},{5,4},{6,5},{7,6},{9,8},{10,9},{11,10},{13,12},{... | collective-permute-start | bytes 55304 | tf_op jit(solution)/shard_map/ppermute | solution.py:21
  274.1 2.6 collective-permute-start.14
  275.4 4.7 %collective-permute-start.15 = (f32[3,1,8,192]{3,2,0,1:T(8,128)S(1)}, f32[3,1,8,192]{3,2,0,1:T(8,128)S(1)}, u32[]{:S(2)}, u32[]{:S(2)}) collective-permute-start(f32[3,1,8,192]{3,2,0,1:T(8,128)S(1)} %get-tuple-element.225), channel_id=1, source_target_pairs={{4,0},{8,4},{12,8},{5,1},{9,5},{13,9},{6,2},{10,6},{14,10},{7,3},{... | collective-permute-start | bytes 55304 | tf_op jit(solution)/shard_map/ppermute | solution.py:21
  281.0 8.0 %all-to-all-start.7 = ((f32[6,3,8,192]{3,2,1,0:T(8,128)}), f32[6,3,8,192]{3,2,1,0:T(8,128)S(1)}, u32[]{:S(2)}, u32[]{:S(2)}) async-start(f32[6,3,8,192]{3,2,1,0:T(8,128)} %broadcast_multiply_fusion), calls=%async_computation.7 | async-start | bytes 294912 | tf_op jit(solution)/shard_map/all_to_all | solution.py:215
  289.0 8.3 %all-to-all-start.6 = ((f32[6,3,8,192]{3,2,1,0:T(8,128)}), f32[6,3,8,192]{3,2,1,0:T(8,128)S(1)}, u32[]{:S(2)}, u32[]{:S(2)}) async-start(f32[6,3,8,192]{3,2,1,0:T(8,128)} %broadcast_multiply_fusion.1), calls=%async_computation.6 | async-start | bytes 294912 | tf_op jit(solution)/shard_map/all_to_all | solution.py:214
  292.4 49.2 %all-reduce.16.cloned.1.call-start = ((), (), s32[]{:S(2)}) async-start(), calls=%async_computation.16 | async-start | bytes 393216
  308.9 35.5 %reduce-scatter.11.cloned.1.call-start = ((), (), s32[]{:S(2)}) async-start(), calls=%async_computation.13 | async-start | bytes 245760 | tf_op jit(solution)/shard_map/reduce_scatter | solution.py:240
Sparse Core Ops, SparseCore 0:
  104.7 35.7 all-reduce.11
  209.3 32.5 all-reduce.13
  309.1 32.5 all-reduce.15
Sparse Core Ops, SparseCore 1:
  107.5 20.6 reduce-scatter.6
  212.1 17.3 reduce-scatter.8
  311.9 17.3 reduce-scatter.10
